TPU v7x, 128 devices: a whole 4x4x4 slice. The times are simulated.
128 devices in a mesh: data: 1, time: 128 (over z, y, x, core).
Axes of the slice: x: 4, y: 4, z: 4, core: 2. Of those that a mesh axis runs over, the one named last changes fastest.
Arguments:
- x_init: float32 [2, 64, 768], P('data')
- w_in: bfloat16 [768, 3072], replicated
- w_out: bfloat16 [3072, 768], replicated
- gamma_c: bfloat16 [1536, 3072], P('time')
- beta_c: bfloat16 [1536, 3072], P('time')
- gamma_u: bfloat16 [1536, 3072], P('time')
- beta_u: bfloat16 [1536, 3072], P('time')
- step_h: float32 [1536], P('time')
- guide_w: float32 [1], replicated
Outputs:
- output: float32 [1536, 2, 64, 768], P('time', 'data')
All inputs are finite; a program needn't handle non-finite values.
Results may differ from a plain program's by a relative error of at most 0.00877005.
Values are sent between devices in bfloat16 or wider.
A program may use at most 1 GiB of HBM per device.

v0:
```python
import jax
import jax.numpy as jnp
import math
from jax import lax
from jax.sharding import PartitionSpec as P

NUM_SWEEPS = 4


def solution(mesh):
    num_time = mesh.shape["time"]
    num_levels = math.ceil(math.log2(num_time))
    shift_perms = [[(src, src + 2 ** level) for src in range(num_time - 2 ** level)] for level in range(num_levels)]

    def local(x_init, w_in, w_out, gamma_c, beta_c, gamma_u, beta_u, step_h, guide_w):
        guide = guide_w[0]
        gain_pair = 1.0 + jnp.stack([gamma_c, gamma_u], axis=0).astype(jnp.float32)
        shift_pair = jnp.stack([beta_c, beta_u], axis=0).astype(jnp.float32)

        def sweep(index, states):
            pre_act = jnp.einsum("kbnc,cd->kbnd", states.astype(jnp.bfloat16), w_in, preferred_element_type=jnp.float32)
            act = jax.nn.gelu(pre_act[None] * gain_pair[:, :, None, None, :] + shift_pair[:, :, None, None, :]).astype(jnp.bfloat16)
            outs = jnp.einsum("ekbnd,dc->ekbnc", act, w_out, preferred_element_type=jnp.float32)
            drift = step_h[:, None, None, None] * ((1.0 + guide) * outs[0] - guide * outs[1])
            running = jnp.cumsum(drift, axis=0)
            dev_total = running[-1]
            prefix = dev_total
            for perm in shift_perms:
                prefix = prefix + lax.ppermute(prefix, "time", perm)
            before = prefix - dev_total
            local_before = jnp.concatenate([jnp.zeros_like(drift[:1]), running[:-1]], axis=0)
            return x_init[None] + (before[None] + local_before)

        start = jnp.broadcast_to(x_init[None], (step_h.shape[0],) + x_init.shape)
        return lax.fori_loop(0, NUM_SWEEPS, sweep, start)

    return jax.shard_map(local, mesh=mesh, in_specs=(P("data", None, None), P(None, None), P(None, None), P("time", None), P("time", None), P("time", None), P("time", None), P("time"), P(None)), out_specs=P("time", "data", None, None), check_vma=False)
```

profile of v0, /device:TPU:0, one launch (start us, length us, event | category | flops | bytes accessed | tf_op | source)
XLA Modules:
  0.0 587.8 jit_solution(7185716229455271478)
XLA Ops:
  6.4 581.4 %while.11 = (s32[]{:T(128)}, f32[12,2,64,768]{3,2,1,0:T(8,128)}, f32[2,64,768]{2,1,0:T(8,128)S(1)}, f32[12]{0:T(128)S(1)}, f32[]{:T(128)}, /*index=5*/bf16[768,3...) while((s32[]{:T(128)}, f32[12,2,64,768]{3,2,1,0:T(8,128)}, ...), condition=%wide.region_2.3_spmd, body=%wide.region_0.2_spmd.sunk | while | flops 21869101056 | bytes 152764944 | solution.py:35
  6.4 14.4 %fusion.48 = f32[12,2,64,3072]{3,2,1,0:T(8,128)} fusion(bf16[768,3072]{1,0:T(8,128)(2,1)} %get-tuple-element.202, f32[12,2,64,768]{3,2,1,0:T(8,128)} %get-tuple-element.187), kind=kOutput, calls=%fused_computation.24.clone.1 | convolution fusion | flops 7248936960 | bytes 28311552 | tf_op jit(solution)/shard_map/while/body/eval_jaxpr/kbnc,cd->kbnd/dot_general | solution.py:21
  20.8 28.3 %fusion.49 = f32[2,12,2,64,768]{4,3,2,1,0:T(8,128)} fusion(f32[2,12,3072]{2,1,0:T(8,128)S(1)} %get-tuple-element.204, f32[2,12,3072]{2,1,0:T(8,128)S(1)} %get-tuple-element.203, f32[12,2,64,3072]{3,2,1,0:T(8,128)} %fusion.48, bf16[3072,768]{1,0:T(8,128)(2,1)S(1)} %copy-done.3), kind=kOutput, calls=%fused_computation.9.clone.1 | convolution fusion | flops 14599323648 | bytes 33619968 | tf_op jit(solution)/shard_map/while/body/eval_jaxpr/ekbnd,dc->ekbnc/dot_general | solution.py:23
  56.8 10.0 %collective-permute-start.1 = (f32[2,64,768]{2,1,0:T(8,128)S(1)}, f32[2,64,768]{2,1,0:T(8,128)S(1)}, u32[]{:S(2)}, u32[]{:S(2)}) collective-permute-start(f32[2,64,768]{2,1,0:T(8,128)S(1)} %fusion.51), channel_id=1, source_target_pairs={{0,2},{1,3},{2,4},{3,5},{4,6},{5,7},{6,8},{7,9},{8,10},{9,11},{10,... | collective-permute-start | bytes 1179656 | tf_op jit(solution)/shard_map/while/body/eval_jaxpr/ppermute | solution.py:29
  66.8 7.6 %collective-permute-done.1 = f32[2,64,768]{2,1,0:T(8,128)S(1)} collective-permute-done((f32[2,64,768]{2,1,0:T(8,128)S(1)}, f32[2,64,768]{2,1,0:T(8,128)S(1)}, u32[]{:S(2)}, u32[]{:S(2)}) %collective-permute-start.1) | collective-permute-done | bytes 393248 | tf_op jit(solution)/shard_map/while/body/eval_jaxpr/ppermute | solution.py:29
  80.1 6.8 %collective-permute-done.2 = f32[2,64,768]{2,1,0:T(8,128)S(1)} collective-permute-done((f32[2,64,768]{2,1,0:T(8,128)S(1)}, f32[2,64,768]{2,1,0:T(8,128)S(1)}, u32[]{:S(2)}, u32[]{:S(2)}) %collective-permute-start.2) | collective-permute-done | bytes 393248 | tf_op jit(solution)/shard_map/while/body/eval_jaxpr/ppermute | solution.py:29
  86.9 6.7 %collective-permute-start.3 = (f32[2,64,768]{2,1,0:T(8,128)S(1)}, f32[2,64,768]{2,1,0:T(8,128)S(1)}, u32[]{:S(2)}, u32[]{:S(2)}) collective-permute-start(f32[2,64,768]{2,1,0:T(8,128)S(1)} %add.150), channel_id=1, source_target_pairs={{0,8},{1,9},{2,10},{3,11},{4,12},{5,13},{6,14},{7,15},{8,16},{9,17... | collective-permute-start | bytes 1179656 | tf_op jit(solution)/shard_map/while/body/eval_jaxpr/ppermute | solution.py:29
  99.0 10.2 %collective-permute-start.4 = (f32[2,64,768]{2,1,0:T(8,128)S(1)}, f32[2,64,768]{2,1,0:T(8,128)S(1)}, u32[]{:S(2)}, u32[]{:S(2)}) collective-permute-start(f32[2,64,768]{2,1,0:T(8,128)S(1)} %add.151), channel_id=1, source_target_pairs={{0,16},{1,17},{2,18},{3,19},{4,20},{5,21},{6,22},{7,23},{8,24},{9,... | collective-permute-start | bytes 1179656 | tf_op jit(solution)/shard_map/while/body/eval_jaxpr/ppermute | solution.py:29
  114.6 13.7 %collective-permute-start.5 = (f32[2,64,768]{2,1,0:T(8,128)S(1)}, f32[2,64,768]{2,1,0:T(8,128)S(1)}, u32[]{:S(2)}, u32[]{:S(2)}) collective-permute-start(f32[2,64,768]{2,1,0:T(8,128)S(1)} %add.152), channel_id=1, source_target_pairs={{0,32},{1,33},{2,34},{3,35},{4,36},{5,37},{6,38},{7,39},{8,40},{9,... | collective-permute-start | bytes 1179656 | tf_op jit(solution)/shard_map/while/body/eval_jaxpr/ppermute | solution.py:29
  151.2 14.4 %fusion.48 = f32[12,2,64,3072]{3,2,1,0:T(8,128)} fusion(bf16[768,3072]{1,0:T(8,128)(2,1)} %get-tuple-element.202, f32[12,2,64,768]{3,2,1,0:T(8,128)} %get-tuple-element.187), kind=kOutput, calls=%fused_computation.24.clone.1 | convolution fusion | flops 7248936960 | bytes 28311552 | tf_op jit(solution)/shard_map/while/body/eval_jaxpr/kbnc,cd->kbnd/dot_general | solution.py:21
  165.7 28.2 %fusion.49 = f32[2,12,2,64,768]{4,3,2,1,0:T(8,128)} fusion(f32[2,12,3072]{2,1,0:T(8,128)S(1)} %get-tuple-element.204, f32[2,12,3072]{2,1,0:T(8,128)S(1)} %get-tuple-element.203, f32[12,2,64,3072]{3,2,1,0:T(8,128)} %fusion.48, bf16[3072,768]{1,0:T(8,128)(2,1)S(1)} %copy-done.3), kind=kOutput, calls=%fused_computation.9.clone.1 | convolution fusion | flops 14599323648 | bytes 33619968 | tf_op jit(solution)/shard_map/while/body/eval_jaxpr/ekbnd,dc->ekbnc/dot_general | solution.py:23
  205.4 7.8 %collective-permute-done.1 = f32[2,64,768]{2,1,0:T(8,128)S(1)} collective-permute-done((f32[2,64,768]{2,1,0:T(8,128)S(1)}, f32[2,64,768]{2,1,0:T(8,128)S(1)}, u32[]{:S(2)}, u32[]{:S(2)}) %collective-permute-start.1) | collective-permute-done | bytes 393248 | tf_op jit(solution)/shard_map/while/body/eval_jaxpr/ppermute | solution.py:29
  218.0 9.5 %collective-permute-done.2 = f32[2,64,768]{2,1,0:T(8,128)S(1)} collective-permute-done((f32[2,64,768]{2,1,0:T(8,128)S(1)}, f32[2,64,768]{2,1,0:T(8,128)S(1)}, u32[]{:S(2)}, u32[]{:S(2)}) %collective-permute-start.2) | collective-permute-done | bytes 393248 | tf_op jit(solution)/shard_map/while/body/eval_jaxpr/ppermute | solution.py:29
  227.5 8.8 %collective-permute-start.3 = (f32[2,64,768]{2,1,0:T(8,128)S(1)}, f32[2,64,768]{2,1,0:T(8,128)S(1)}, u32[]{:S(2)}, u32[]{:S(2)}) collective-permute-start(f32[2,64,768]{2,1,0:T(8,128)S(1)} %add.150), channel_id=1, source_target_pairs={{0,8},{1,9},{2,10},{3,11},{4,12},{5,13},{6,14},{7,15},{8,16},{9,17... | collective-permute-start | bytes 1179656 | tf_op jit(solution)/shard_map/while/body/eval_jaxpr/ppermute | solution.py:29
  236.3 6.7 %collective-permute-done.3 = f32[2,64,768]{2,1,0:T(8,128)S(1)} collective-permute-done((f32[2,64,768]{2,1,0:T(8,128)S(1)}, f32[2,64,768]{2,1,0:T(8,128)S(1)}, u32[]{:S(2)}, u32[]{:S(2)}) %collective-permute-start.3) | collective-permute-done | bytes 393248 | tf_op jit(solution)/shard_map/while/body/eval_jaxpr/ppermute | solution.py:29
  251.9 20.2 %collective-permute-start.5 = (f32[2,64,768]{2,1,0:T(8,128)S(1)}, f32[2,64,768]{2,1,0:T(8,128)S(1)}, u32[]{:S(2)}, u32[]{:S(2)}) collective-permute-start(f32[2,64,768]{2,1,0:T(8,128)S(1)} %add.152), channel_id=1, source_target_pairs={{0,32},{1,33},{2,34},{3,35},{4,36},{5,37},{6,38},{7,39},{8,40},{9,... | collective-permute-start | bytes 1179656 | tf_op jit(solution)/shard_map/while/body/eval_jaxpr/ppermute | solution.py:29
  278.4 6.8 %collective-permute-start.6 = (f32[2,64,768]{2,1,0:T(8,128)S(1)}, f32[2,64,768]{2,1,0:T(8,128)S(1)}, u32[]{:S(2)}, u32[]{:S(2)}) collective-permute-start(f32[2,64,768]{2,1,0:T(8,128)S(1)} %add.153), channel_id=1, source_target_pairs={{0,64},{1,65},{2,66},{3,67},{4,68},{5,69},{6,70},{7,71},{8,72},{9,... | collective-permute-start | bytes 1179656 | tf_op jit(solution)/shard_map/while/body/eval_jaxpr/ppermute | solution.py:29
  296.5 14.4 %fusion.48 = f32[12,2,64,3072]{3,2,1,0:T(8,128)} fusion(bf16[768,3072]{1,0:T(8,128)(2,1)} %get-tuple-element.202, f32[12,2,64,768]{3,2,1,0:T(8,128)} %get-tuple-element.187), kind=kOutput, calls=%fused_computation.24.clone.1 | convolution fusion | flops 7248936960 | bytes 28311552 | tf_op jit(solution)/shard_map/while/body/eval_jaxpr/kbnc,cd->kbnd/dot_general | solution.py:21
  311.0 28.3 %fusion.49 = f32[2,12,2,64,768]{4,3,2,1,0:T(8,128)} fusion(f32[2,12,3072]{2,1,0:T(8,128)S(1)} %get-tuple-element.204, f32[2,12,3072]{2,1,0:T(8,128)S(1)} %get-tuple-element.203, f32[12,2,64,3072]{3,2,1,0:T(8,128)} %fusion.48, bf16[3072,768]{1,0:T(8,128)(2,1)S(1)} %copy-done.3), kind=kOutput, calls=%fused_computation.9.clone.1 | convolution fusion | flops 14599323648 | bytes 33619968 | tf_op jit(solution)/shard_map/while/body/eval_jaxpr/ekbnd,dc->ekbnc/dot_general | solution.py:23
  346.9 8.0 %collective-permute-start.1 = (f32[2,64,768]{2,1,0:T(8,128)S(1)}, f32[2,64,768]{2,1,0:T(8,128)S(1)}, u32[]{:S(2)}, u32[]{:S(2)}) collective-permute-start(f32[2,64,768]{2,1,0:T(8,128)S(1)} %fusion.51), channel_id=1, source_target_pairs={{0,2},{1,3},{2,4},{3,5},{4,6},{5,7},{6,8},{7,9},{8,10},{9,11},{10,... | collective-permute-start | bytes 1179656 | tf_op jit(solution)/shard_map/while/body/eval_jaxpr/ppermute | solution.py:29
  382.7 12.6 %collective-permute-start.4 = (f32[2,64,768]{2,1,0:T(8,128)S(1)}, f32[2,64,768]{2,1,0:T(8,128)S(1)}, u32[]{:S(2)}, u32[]{:S(2)}) collective-permute-start(f32[2,64,768]{2,1,0:T(8,128)S(1)} %add.151), channel_id=1, source_target_pairs={{0,16},{1,17},{2,18},{3,19},{4,20},{5,21},{6,22},{7,23},{8,24},{9,... | collective-permute-start | bytes 1179656 | tf_op jit(solution)/shard_map/while/body/eval_jaxpr/ppermute | solution.py:29
  400.7 16.2 %collective-permute-start.5 = (f32[2,64,768]{2,1,0:T(8,128)S(1)}, f32[2,64,768]{2,1,0:T(8,128)S(1)}, u32[]{:S(2)}, u32[]{:S(2)}) collective-permute-start(f32[2,64,768]{2,1,0:T(8,128)S(1)} %add.152), channel_id=1, source_target_pairs={{0,32},{1,33},{2,34},{3,35},{4,36},{5,37},{6,38},{7,39},{8,40},{9,... | collective-permute-start | bytes 1179656 | tf_op jit(solution)/shard_map/while/body/eval_jaxpr/ppermute | solution.py:29
  416.9 6.7 %collective-permute-done.5 = f32[2,64,768]{2,1,0:T(8,128)S(1)} collective-permute-done((f32[2,64,768]{2,1,0:T(8,128)S(1)}, f32[2,64,768]{2,1,0:T(8,128)S(1)}, u32[]{:S(2)}, u32[]{:S(2)}) %collective-permute-start.5) | collective-permute-done | bytes 393248 | tf_op jit(solution)/shard_map/while/body/eval_jaxpr/ppermute | solution.py:29
  423.7 7.0 %collective-permute-start.6 = (f32[2,64,768]{2,1,0:T(8,128)S(1)}, f32[2,64,768]{2,1,0:T(8,128)S(1)}, u32[]{:S(2)}, u32[]{:S(2)}) collective-permute-start(f32[2,64,768]{2,1,0:T(8,128)S(1)} %add.153), channel_id=1, source_target_pairs={{0,64},{1,65},{2,66},{3,67},{4,68},{5,69},{6,70},{7,71},{8,72},{9,... | collective-permute-start | bytes 1179656 | tf_op jit(solution)/shard_map/while/body/eval_jaxpr/ppermute | solution.py:29
  442.0 14.4 %fusion.48 = f32[12,2,64,3072]{3,2,1,0:T(8,128)} fusion(bf16[768,3072]{1,0:T(8,128)(2,1)} %get-tuple-element.202, f32[12,2,64,768]{3,2,1,0:T(8,128)} %get-tuple-element.187), kind=kOutput, calls=%fused_computation.24.clone.1 | convolution fusion | flops 7248936960 | bytes 28311552 | tf_op jit(solution)/shard_map/while/body/eval_jaxpr/kbnc,cd->kbnd/dot_general | solution.py:21
  456.4 28.3 %fusion.49 = f32[2,12,2,64,768]{4,3,2,1,0:T(8,128)} fusion(f32[2,12,3072]{2,1,0:T(8,128)S(1)} %get-tuple-element.204, f32[2,12,3072]{2,1,0:T(8,128)S(1)} %get-tuple-element.203, f32[12,2,64,3072]{3,2,1,0:T(8,128)} %fusion.48, bf16[3072,768]{1,0:T(8,128)(2,1)S(1)} %copy-done.3), kind=kOutput, calls=%fused_computation.9.clone.1 | convolution fusion | flops 14599323648 | bytes 33619968 | tf_op jit(solution)/shard_map/while/body/eval_jaxpr/ekbnd,dc->ekbnc/dot_general | solution.py:23
  492.4 7.9 %collective-permute-start.1 = (f32[2,64,768]{2,1,0:T(8,128)S(1)}, f32[2,64,768]{2,1,0:T(8,128)S(1)}, u32[]{:S(2)}, u32[]{:S(2)}) collective-permute-start(f32[2,64,768]{2,1,0:T(8,128)S(1)} %fusion.51), channel_id=1, source_target_pairs={{0,2},{1,3},{2,4},{3,5},{4,6},{5,7},{6,8},{7,9},{8,10},{9,11},{10,... | collective-permute-start | bytes 1179656 | tf_op jit(solution)/shard_map/while/body/eval_jaxpr/ppermute | solution.py:29
  516.1 6.6 %collective-permute-start.3 = (f32[2,64,768]{2,1,0:T(8,128)S(1)}, f32[2,64,768]{2,1,0:T(8,128)S(1)}, u32[]{:S(2)}, u32[]{:S(2)}) collective-permute-start(f32[2,64,768]{2,1,0:T(8,128)S(1)} %add.150), channel_id=1, source_target_pairs={{0,8},{1,9},{2,10},{3,11},{4,12},{5,13},{6,14},{7,15},{8,16},{9,17... | collective-permute-start | bytes 1179656 | tf_op jit(solution)/shard_map/while/body/eval_jaxpr/ppermute | solution.py:29
  528.0 12.4 %collective-permute-start.4 = (f32[2,64,768]{2,1,0:T(8,128)S(1)}, f32[2,64,768]{2,1,0:T(8,128)S(1)}, u32[]{:S(2)}, u32[]{:S(2)}) collective-permute-start(f32[2,64,768]{2,1,0:T(8,128)S(1)} %add.151), channel_id=1, source_target_pairs={{0,16},{1,17},{2,18},{3,19},{4,20},{5,21},{6,22},{7,23},{8,24},{9,... | collective-permute-start | bytes 1179656 | tf_op jit(solution)/shard_map/while/body/eval_jaxpr/ppermute | solution.py:29
  545.7 16.0 %collective-permute-start.5 = (f32[2,64,768]{2,1,0:T(8,128)S(1)}, f32[2,64,768]{2,1,0:T(8,128)S(1)}, u32[]{:S(2)}, u32[]{:S(2)}) collective-permute-start(f32[2,64,768]{2,1,0:T(8,128)S(1)} %add.152), channel_id=1, source_target_pairs={{0,32},{1,33},{2,34},{3,35},{4,36},{5,37},{6,38},{7,39},{8,40},{9,... | collective-permute-start | bytes 1179656 | tf_op jit(solution)/shard_map/while/body/eval_jaxpr/ppermute | solution.py:29
  561.8 7.3 %collective-permute-done.5 = f32[2,64,768]{2,1,0:T(8,128)S(1)} collective-permute-done((f32[2,64,768]{2,1,0:T(8,128)S(1)}, f32[2,64,768]{2,1,0:T(8,128)S(1)}, u32[]{:S(2)}, u32[]{:S(2)}) %collective-permute-start.5) | collective-permute-done | bytes 393248 | tf_op jit(solution)/shard_map/while/body/eval_jaxpr/ppermute | solution.py:29
  569.1 7.3 %collective-permute-start.6 = (f32[2,64,768]{2,1,0:T(8,128)S(1)}, f32[2,64,768]{2,1,0:T(8,128)S(1)}, u32[]{:S(2)}, u32[]{:S(2)}) collective-permute-start(f32[2,64,768]{2,1,0:T(8,128)S(1)} %add.153), channel_id=1, source_target_pairs={{0,64},{1,65},{2,66},{3,67},{4,68},{5,69},{6,70},{7,71},{8,72},{9,... | collective-permute-start | bytes 1179656 | tf_op jit(solution)/shard_map/while/body/eval_jaxpr/ppermute | solution.py:29
  (100 shorter events, 192.9 us)
Async XLA Ops:
  54.0 88.3 %copy-start = (f32[12,2,64,768]{3,2,1,0:T(8,128)}, f32[12,2,64,768]{3,2,1,0:T(8,128)S(1)}, u32[]{:S(2)}) copy-start(f32[12,2,64,768]{3,2,1,0:T(8,128)S(1)} %fusion.50) | copy-start | bytes 14155780 | tf_op jit(solution)/shard_map/while
  54.1 2.6 collective-permute-start
  56.8 17.6 %collective-permute-start.1 = (f32[2,64,768]{2,1,0:T(8,128)S(1)}, f32[2,64,768]{2,1,0:T(8,128)S(1)}, u32[]{:S(2)}, u32[]{:S(2)}) collective-permute-start(f32[2,64,768]{2,1,0:T(8,128)S(1)} %fusion.51), channel_id=1, source_target_pairs={{0,2},{1,3},{2,4},{3,5},{4,6},{5,7},{6,8},{7,9},{8,10},{9,11},{10,... | collective-permute-start | bytes 1179656 | tf_op jit(solution)/shard_map/while/body/eval_jaxpr/ppermute | solution.py:29
  74.4 12.5 %collective-permute-start.2 = (f32[2,64,768]{2,1,0:T(8,128)S(1)}, f32[2,64,768]{2,1,0:T(8,128)S(1)}, u32[]{:S(2)}, u32[]{:S(2)}) collective-permute-start(f32[2,64,768]{2,1,0:T(8,128)S(1)} %add.149), channel_id=1, source_target_pairs={{0,4},{1,5},{2,6},{3,7},{4,8},{5,9},{6,10},{7,11},{8,12},{9,13},{1... | collective-permute-start | bytes 1179656 | tf_op jit(solution)/shard_map/while/body/eval_jaxpr/ppermute | solution.py:29
  86.9 12.0 %collective-permute-start.3 = (f32[2,64,768]{2,1,0:T(8,128)S(1)}, f32[2,64,768]{2,1,0:T(8,128)S(1)}, u32[]{:S(2)}, u32[]{:S(2)}) collective-permute-start(f32[2,64,768]{2,1,0:T(8,128)S(1)} %add.150), channel_id=1, source_target_pairs={{0,8},{1,9},{2,10},{3,11},{4,12},{5,13},{6,14},{7,15},{8,16},{9,17... | collective-permute-start | bytes 1179656 | tf_op jit(solution)/shard_map/while/body/eval_jaxpr/ppermute | solution.py:29
  99.0 15.5 %collective-permute-start.4 = (f32[2,64,768]{2,1,0:T(8,128)S(1)}, f32[2,64,768]{2,1,0:T(8,128)S(1)}, u32[]{:S(2)}, u32[]{:S(2)}) collective-permute-start(f32[2,64,768]{2,1,0:T(8,128)S(1)} %add.151), channel_id=1, source_target_pairs={{0,16},{1,17},{2,18},{3,19},{4,20},{5,21},{6,22},{7,23},{8,24},{9,... | collective-permute-start | bytes 1179656 | tf_op jit(solution)/shard_map/while/body/eval_jaxpr/ppermute | solution.py:29
  114.6 18.9 %collective-permute-start.5 = (f32[2,64,768]{2,1,0:T(8,128)S(1)}, f32[2,64,768]{2,1,0:T(8,128)S(1)}, u32[]{:S(2)}, u32[]{:S(2)}) collective-permute-start(f32[2,64,768]{2,1,0:T(8,128)S(1)} %add.152), channel_id=1, source_target_pairs={{0,32},{1,33},{2,34},{3,35},{4,36},{5,37},{6,38},{7,39},{8,40},{9,... | collective-permute-start | bytes 1179656 | tf_op jit(solution)/shard_map/while/body/eval_jaxpr/ppermute | solution.py:29
  133.5 11.6 %collective-permute-start.6 = (f32[2,64,768]{2,1,0:T(8,128)S(1)}, f32[2,64,768]{2,1,0:T(8,128)S(1)}, u32[]{:S(2)}, u32[]{:S(2)}) collective-permute-start(f32[2,64,768]{2,1,0:T(8,128)S(1)} %add.153), channel_id=1, source_target_pairs={{0,64},{1,65},{2,66},{3,67},{4,68},{5,69},{6,70},{7,71},{8,72},{9,... | collective-permute-start | bytes 1179656 | tf_op jit(solution)/shard_map/while/body/eval_jaxpr/ppermute | solution.py:29
  198.9 88.8 %copy-start = (f32[12,2,64,768]{3,2,1,0:T(8,128)}, f32[12,2,64,768]{3,2,1,0:T(8,128)S(1)}, u32[]{:S(2)}) copy-start(f32[12,2,64,768]{3,2,1,0:T(8,128)S(1)} %fusion.50) | copy-start | bytes 14155780 | tf_op jit(solution)/shard_map/while
  198.9 2.6 collective-permute-start
  201.6 11.6 %collective-permute-start.1 = (f32[2,64,768]{2,1,0:T(8,128)S(1)}, f32[2,64,768]{2,1,0:T(8,128)S(1)}, u32[]{:S(2)}, u32[]{:S(2)}) collective-permute-start(f32[2,64,768]{2,1,0:T(8,128)S(1)} %fusion.51), channel_id=1, source_target_pairs={{0,2},{1,3},{2,4},{3,5},{4,6},{5,7},{6,8},{7,9},{8,10},{9,11},{10,... | collective-permute-start | bytes 1179656 | tf_op jit(solution)/shard_map/while/body/eval_jaxpr/ppermute | solution.py:29
  213.2 14.2 %collective-permute-start.2 = (f32[2,64,768]{2,1,0:T(8,128)S(1)}, f32[2,64,768]{2,1,0:T(8,128)S(1)}, u32[]{:S(2)}, u32[]{:S(2)}) collective-permute-start(f32[2,64,768]{2,1,0:T(8,128)S(1)} %add.149), channel_id=1, source_target_pairs={{0,4},{1,5},{2,6},{3,7},{4,8},{5,9},{6,10},{7,11},{8,12},{9,13},{1... | collective-permute-start | bytes 1179656 | tf_op jit(solution)/shard_map/while/body/eval_jaxpr/ppermute | solution.py:29
  227.5 15.5 %collective-permute-start.3 = (f32[2,64,768]{2,1,0:T(8,128)S(1)}, f32[2,64,768]{2,1,0:T(8,128)S(1)}, u32[]{:S(2)}, u32[]{:S(2)}) collective-permute-start(f32[2,64,768]{2,1,0:T(8,128)S(1)} %add.150), channel_id=1, source_target_pairs={{0,8},{1,9},{2,10},{3,11},{4,12},{5,13},{6,14},{7,15},{8,16},{9,17... | collective-permute-start | bytes 1179656 | tf_op jit(solution)/shard_map/while/body/eval_jaxpr/ppermute | solution.py:29
  243.1 8.7 %collective-permute-start.4 = (f32[2,64,768]{2,1,0:T(8,128)S(1)}, f32[2,64,768]{2,1,0:T(8,128)S(1)}, u32[]{:S(2)}, u32[]{:S(2)}) collective-permute-start(f32[2,64,768]{2,1,0:T(8,128)S(1)} %add.151), channel_id=1, source_target_pairs={{0,16},{1,17},{2,18},{3,19},{4,20},{5,21},{6,22},{7,23},{8,24},{9,... | collective-permute-start | bytes 1179656 | tf_op jit(solution)/shard_map/while/body/eval_jaxpr/ppermute | solution.py:29
  251.9 26.5 %collective-permute-start.5 = (f32[2,64,768]{2,1,0:T(8,128)S(1)}, f32[2,64,768]{2,1,0:T(8,128)S(1)}, u32[]{:S(2)}, u32[]{:S(2)}) collective-permute-start(f32[2,64,768]{2,1,0:T(8,128)S(1)} %add.152), channel_id=1, source_target_pairs={{0,32},{1,33},{2,34},{3,35},{4,36},{5,37},{6,38},{7,39},{8,40},{9,... | collective-permute-start | bytes 1179656 | tf_op jit(solution)/shard_map/while/body/eval_jaxpr/ppermute | solution.py:29
  278.4 12.1 %collective-permute-start.6 = (f32[2,64,768]{2,1,0:T(8,128)S(1)}, f32[2,64,768]{2,1,0:T(8,128)S(1)}, u32[]{:S(2)}, u32[]{:S(2)}) collective-permute-start(f32[2,64,768]{2,1,0:T(8,128)S(1)} %add.153), channel_id=1, source_target_pairs={{0,64},{1,65},{2,66},{3,67},{4,68},{5,69},{6,70},{7,71},{8,72},{9,... | collective-permute-start | bytes 1179656 | tf_op jit(solution)/shard_map/while/body/eval_jaxpr/ppermute | solution.py:29
  344.2 88.9 %copy-start = (f32[12,2,64,768]{3,2,1,0:T(8,128)}, f32[12,2,64,768]{3,2,1,0:T(8,128)S(1)}, u32[]{:S(2)}) copy-start(f32[12,2,64,768]{3,2,1,0:T(8,128)S(1)} %fusion.50) | copy-start | bytes 14155780 | tf_op jit(solution)/shard_map/while
  344.2 2.6 collective-permute-start
  346.9 13.8 %collective-permute-start.1 = (f32[2,64,768]{2,1,0:T(8,128)S(1)}, f32[2,64,768]{2,1,0:T(8,128)S(1)}, u32[]{:S(2)}, u32[]{:S(2)}) collective-permute-start(f32[2,64,768]{2,1,0:T(8,128)S(1)} %fusion.51), channel_id=1, source_target_pairs={{0,2},{1,3},{2,4},{3,5},{4,6},{5,7},{6,8},{7,9},{8,10},{9,11},{10,... | collective-permute-start | bytes 1179656 | tf_op jit(solution)/shard_map/while/body/eval_jaxpr/ppermute | solution.py:29
  360.8 10.2 %collective-permute-start.2 = (f32[2,64,768]{2,1,0:T(8,128)S(1)}, f32[2,64,768]{2,1,0:T(8,128)S(1)}, u32[]{:S(2)}, u32[]{:S(2)}) collective-permute-start(f32[2,64,768]{2,1,0:T(8,128)S(1)} %add.149), channel_id=1, source_target_pairs={{0,4},{1,5},{2,6},{3,7},{4,8},{5,9},{6,10},{7,11},{8,12},{9,13},{1... | collective-permute-start | bytes 1179656 | tf_op jit(solution)/shard_map/while/body/eval_jaxpr/ppermute | solution.py:29
  371.0 11.6 %collective-permute-start.3 = (f32[2,64,768]{2,1,0:T(8,128)S(1)}, f32[2,64,768]{2,1,0:T(8,128)S(1)}, u32[]{:S(2)}, u32[]{:S(2)}) collective-permute-start(f32[2,64,768]{2,1,0:T(8,128)S(1)} %add.150), channel_id=1, source_target_pairs={{0,8},{1,9},{2,10},{3,11},{4,12},{5,13},{6,14},{7,15},{8,16},{9,17... | collective-permute-start | bytes 1179656 | tf_op jit(solution)/shard_map/while/body/eval_jaxpr/ppermute | solution.py:29
  382.7 17.9 %collective-permute-start.4 = (f32[2,64,768]{2,1,0:T(8,128)S(1)}, f32[2,64,768]{2,1,0:T(8,128)S(1)}, u32[]{:S(2)}, u32[]{:S(2)}) collective-permute-start(f32[2,64,768]{2,1,0:T(8,128)S(1)} %add.151), channel_id=1, source_target_pairs={{0,16},{1,17},{2,18},{3,19},{4,20},{5,21},{6,22},{7,23},{8,24},{9,... | collective-permute-start | bytes 1179656 | tf_op jit(solution)/shard_map/while/body/eval_jaxpr/ppermute | solution.py:29
  400.7 23.0 %collective-permute-start.5 = (f32[2,64,768]{2,1,0:T(8,128)S(1)}, f32[2,64,768]{2,1,0:T(8,128)S(1)}, u32[]{:S(2)}, u32[]{:S(2)}) collective-permute-start(f32[2,64,768]{2,1,0:T(8,128)S(1)} %add.152), channel_id=1, source_target_pairs={{0,32},{1,33},{2,34},{3,35},{4,36},{5,37},{6,38},{7,39},{8,40},{9,... | collective-permute-start | bytes 1179656 | tf_op jit(solution)/shard_map/while/body/eval_jaxpr/ppermute | solution.py:29
  423.7 12.2 %collective-permute-start.6 = (f32[2,64,768]{2,1,0:T(8,128)S(1)}, f32[2,64,768]{2,1,0:T(8,128)S(1)}, u32[]{:S(2)}, u32[]{:S(2)}) collective-permute-start(f32[2,64,768]{2,1,0:T(8,128)S(1)} %add.153), channel_id=1, source_target_pairs={{0,64},{1,65},{2,66},{3,67},{4,68},{5,69},{6,70},{7,71},{8,72},{9,... | collective-permute-start | bytes 1179656 | tf_op jit(solution)/shard_map/while/body/eval_jaxpr/ppermute | solution.py:29
  489.6 89.2 %copy-start = (f32[12,2,64,768]{3,2,1,0:T(8,128)}, f32[12,2,64,768]{3,2,1,0:T(8,128)S(1)}, u32[]{:S(2)}) copy-start(f32[12,2,64,768]{3,2,1,0:T(8,128)S(1)} %fusion.50) | copy-start | bytes 14155780 | tf_op jit(solution)/shard_map/while
  489.7 2.6 collective-permute-start
  492.4 13.6 %collective-permute-start.1 = (f32[2,64,768]{2,1,0:T(8,128)S(1)}, f32[2,64,768]{2,1,0:T(8,128)S(1)}, u32[]{:S(2)}, u32[]{:S(2)}) collective-permute-start(f32[2,64,768]{2,1,0:T(8,128)S(1)} %fusion.51), channel_id=1, source_target_pairs={{0,2},{1,3},{2,4},{3,5},{4,6},{5,7},{6,8},{7,9},{8,10},{9,11},{10,... | collective-permute-start | bytes 1179656 | tf_op jit(solution)/shard_map/while/body/eval_jaxpr/ppermute | solution.py:29
  506.1 10.0 %collective-permute-start.2 = (f32[2,64,768]{2,1,0:T(8,128)S(1)}, f32[2,64,768]{2,1,0:T(8,128)S(1)}, u32[]{:S(2)}, u32[]{:S(2)}) collective-permute-start(f32[2,64,768]{2,1,0:T(8,128)S(1)} %add.149), channel_id=1, source_target_pairs={{0,4},{1,5},{2,6},{3,7},{4,8},{5,9},{6,10},{7,11},{8,12},{9,13},{1... | collective-permute-start | bytes 1179656 | tf_op jit(solution)/shard_map/while/body/eval_jaxpr/ppermute | solution.py:29
  516.1 11.9 %collective-permute-start.3 = (f32[2,64,768]{2,1,0:T(8,128)S(1)}, f32[2,64,768]{2,1,0:T(8,128)S(1)}, u32[]{:S(2)}, u32[]{:S(2)}) collective-permute-start(f32[2,64,768]{2,1,0:T(8,128)S(1)} %add.150), channel_id=1, source_target_pairs={{0,8},{1,9},{2,10},{3,11},{4,12},{5,13},{6,14},{7,15},{8,16},{9,17... | collective-permute-start | bytes 1179656 | tf_op jit(solution)/shard_map/while/body/eval_jaxpr/ppermute | solution.py:29
  528.0 17.7 %collective-permute-start.4 = (f32[2,64,768]{2,1,0:T(8,128)S(1)}, f32[2,64,768]{2,1,0:T(8,128)S(1)}, u32[]{:S(2)}, u32[]{:S(2)}) collective-permute-start(f32[2,64,768]{2,1,0:T(8,128)S(1)} %add.151), channel_id=1, source_target_pairs={{0,16},{1,17},{2,18},{3,19},{4,20},{5,21},{6,22},{7,23},{8,24},{9,... | collective-permute-start | bytes 1179656 | tf_op jit(solution)/shard_map/while/body/eval_jaxpr/ppermute | solution.py:29
  545.7 23.4 %collective-permute-start.5 = (f32[2,64,768]{2,1,0:T(8,128)S(1)}, f32[2,64,768]{2,1,0:T(8,128)S(1)}, u32[]{:S(2)}, u32[]{:S(2)}) collective-permute-start(f32[2,64,768]{2,1,0:T(8,128)S(1)} %add.152), channel_id=1, source_target_pairs={{0,32},{1,33},{2,34},{3,35},{4,36},{5,37},{6,38},{7,39},{8,40},{9,... | collective-permute-start | bytes 1179656 | tf_op jit(solution)/shard_map/while/body/eval_jaxpr/ppermute | solution.py:29
  569.1 12.5 %collective-permute-start.6 = (f32[2,64,768]{2,1,0:T(8,128)S(1)}, f32[2,64,768]{2,1,0:T(8,128)S(1)}, u32[]{:S(2)}, u32[]{:S(2)}) collective-permute-start(f32[2,64,768]{2,1,0:T(8,128)S(1)} %add.153), channel_id=1, source_target_pairs={{0,64},{1,65},{2,66},{3,67},{4,68},{5,69},{6,70},{7,71},{8,72},{9,... | collective-permute-start | bytes 1179656 | tf_op jit(solution)/shard_map/while/body/eval_jaxpr/ppermute | solution.py:29
  (6 other events, 70.4 us)
where the time goes:
time: 589 us; the launch traced here: 588 us
  starting transfers between devices  214 us (36%)
  matrix products  171 us (29%)
  waiting for transfers between devices  141 us (24%)
  other arithmetic  47.3 us (8%)
  local copies, waits for them, and re-layouts  13.6 us (2%)
    ppermute x28, starting transfers between devices, sweep(): prefix = prefix + lax.ppermute(prefix, 'time', perm)  214 us
    ppermute x28, waiting for transfers between devices, sweep(): prefix = prefix + lax.ppermute(prefix, 'time', perm)  141 us
    dot_general x4, matrix products, sweep(): jnp.einsum('ekbnd,dc->ekbnc', act, w_out, preferred_element_type=jnp.floa...  113 us
    dot_general x4, matrix products, sweep(): jnp.einsum('kbnc,cd->kbnd', states.astype(jnp.bfloat16), w_in, preferred_...  57.7 us
    add x4, other arithmetic, sweep(): return x_init[None] + (before[None] + local_before)  20 us
    another operation x4, other arithmetic, sweep(): running = jnp.cumsum(drift, axis=0)  19.8 us
  transfers between devices with their start and end apart: 28, of which 28 were waited for; matrix products, arithmetic and copies ran while one was open for 2% of the time, Pallas kernels for 0%

commit v1 on v0

v1 whole, which is shorter than its diff:
```python
import functools
import math

import jax
import jax.numpy as jnp
from jax import lax
from jax.experimental import pallas as pl
from jax.experimental.pallas import tpu as pltpu
from jax.sharding import PartitionSpec as P

NUM_SWEEPS = 4
CHUNKS = 4
HID_TILE = 256
MESH = pl.DeviceIdType.MESH
GELU_SLOPE = 2.0 * math.sqrt(2.0 / math.pi)
GELU_CUBIC = 4.0 * GELU_SLOPE * 0.044715


def gelu_of_half(half):
    inner = half * (half * half * GELU_CUBIC + GELU_SLOPE)
    return half + half * jnp.tanh(inner)


def sampler(dims, x_ref, w_in, w_out, gamma_c, beta_c, gamma_u, beta_u, step_ref, guide_ref, out_ref,
            local, sib_local, before, sib_before, state, act, first_pre, gains, sib_mod, coef, own_coef, sib_coef,
            tx, rx, send_sem, recv_sem, mod_send, mod_recv, coef_send, coef_recv, loc_send, loc_recv, bef_send, bef_recv):
    steps, rows, channels, hidden, side = dims
    both = 2 * steps
    tall = both * rows
    index = lax.axis_index("time")
    core = lax.rem(index, 2)
    chip = lax.div(index, 2)
    sibling = index + 1 - 2 * core
    coords = (lax.rem(chip, side), lax.rem(lax.div(chip, side), side), lax.div(chip, side * side))
    strides = (2, 2 * side, 2 * side * side)

    def at(target):
        return {"time": target}

    def peer(phase, hop):
        return index + (lax.rem(coords[phase] + hop, side) - coords[phase]) * strides[phase]

    barrier = pltpu.get_barrier_semaphore()
    pl.semaphore_signal(barrier, inc=1, device_id=at(sibling), device_id_type=MESH)
    for phase in range(3):
        for hop in range(1, side):
            pl.semaphore_signal(barrier, inc=1, device_id=at(peer(phase, hop)), device_id_type=MESH)
    pl.semaphore_wait(barrier, 1 + 3 * (side - 1))

    mods = (gamma_c, beta_c, gamma_u, beta_u)
    mod_copies = [pltpu.make_async_remote_copy(src_ref=mods[i], dst_ref=sib_mod.at[i], send_sem=mod_send.at[i], recv_sem=mod_recv.at[i], device_id=at(sibling), device_id_type=MESH) for i in range(4)]
    for copy in mod_copies:
        copy.start()
    guide = guide_ref[0]
    for j in range(steps):
        own_coef[0, j:j + 1, :] = jnp.full((1, channels), step_ref[j] * (1.0 + guide), jnp.float32)
        own_coef[1, j:j + 1, :] = jnp.full((1, channels), step_ref[j] * guide, jnp.float32)
    coef_copy = pltpu.make_async_remote_copy(src_ref=own_coef, dst_ref=sib_coef, send_sem=coef_send, recv_sem=coef_recv, device_id=at(sibling), device_id_type=MESH)

    x_rows = x_ref[core].astype(jnp.bfloat16)
    for tile in range(hidden // HID_TILE):
        cols = slice(tile * HID_TILE, (tile + 1) * HID_TILE)
        first_pre[:, cols] = jnp.dot(x_rows, w_in[:, cols], preferred_element_type=jnp.float32)
    coef_copy.start()

    first = core == 0
    for copy in mod_copies:
        copy.wait()
    for i in range(4):
        mine = mods[i][...].astype(jnp.float32)
        theirs = sib_mod[i].astype(jnp.float32)
        if i % 2 == 0:
            mine, theirs = 0.5 + 0.5 * mine, 0.5 + 0.5 * theirs
        else:
            mine, theirs = 0.5 * mine, 0.5 * theirs
        gains[i, 0:steps, :] = jnp.where(first, mine, theirs)
        gains[i, steps:both, :] = jnp.where(first, theirs, mine)
    coef_copy.wait()
    for i in range(2):
        coef[i, 0:steps, :] = jnp.where(first, own_coef[i], sib_coef[i])
        coef[i, steps:both, :] = jnp.where(first, sib_coef[i], own_coef[i])

    def copies(phase, chunk, turn):
        return [pltpu.make_async_remote_copy(
            src_ref=tx.at[phase, turn], dst_ref=rx.at[phase, chunk, hop - 1], send_sem=send_sem.at[phase, turn, hop - 1],
            recv_sem=recv_sem.at[phase, chunk, hop - 1], device_id=at(peer(phase, hop)), device_id_type=MESH) for hop in range(1, side)]

    def send(phase, chunk, turn):
        for copy in copies(phase, chunk, turn):
            copy.start()

    def finish(phase, chunk, turn):
        for copy in copies(phase, chunk, turn):
            copy.wait()
        lower = jnp.zeros((rows, channels), jnp.float32)
        total = tx[phase, turn]
        for hop in range(1, side):
            part = rx[phase, chunk, hop - 1]
            total = total + part
            lower = lower + jnp.where(coords[phase] >= hop, part, 0.0)
        before[chunk] = lower if phase == 0 else before[chunk] + lower
        if phase < 2:
            tx[phase + 1, turn] = total
            send(phase + 1, chunk, turn)

    def drifts(chunk):
        outs = jnp.dot(act[...], w_out[...], preferred_element_type=jnp.float32)
        run = jnp.zeros((rows, channels), jnp.float32)
        for j in range(both):
            local[chunk, j] = run
            run = run + (outs[j * rows:(j + 1) * rows] * coef[0, j:j + 1, :] - outs[tall + j * rows:tall + (j + 1) * rows] * coef[1, j:j + 1, :])
        return run

    def activate(pre, j, cols):
        for branch in range(2):
            half = pre * gains[2 * branch, j:j + 1, cols] + gains[2 * branch + 1, j:j + 1, cols]
            start = branch * tall + j * rows
            act[start:start + rows, cols] = gelu_of_half(half).astype(jnp.bfloat16)

    def exchange(turn_now, last, step_index):
        for phase in range(3):
            lag = phase + 1

            def one(phase=phase, lag=lag):
                older = step_index - lag
                finish(phase, lax.rem(older, CHUNKS), lax.rem(older, 2))
            if last:
                one()
            else:
                pl.when(step_index >= lag)(one)

    def first_chunk(step_index, carry):
        chunk = step_index
        turn = lax.rem(step_index, 2)
        top = pl.multiple_of(chunk * rows, rows)
        for tile in range(hidden // HID_TILE):
            cols = slice(tile * HID_TILE, (tile + 1) * HID_TILE)
            pre = first_pre[pl.ds(top, rows), cols]
            for j in range(both):
                activate(pre, j, cols)
        tx[0, turn] = drifts(chunk)
        send(0, chunk, turn)
        exchange(turn, False, step_index)
        return carry

    def later_chunk(step_index, carry):
        chunk = lax.rem(step_index, CHUNKS)
        turn = lax.rem(step_index, 2)
        top = pl.multiple_of(chunk * rows, rows)
        base = x_ref[core, pl.ds(top, rows), :] + before[chunk]
        for j in range(both):
            state[j * rows:(j + 1) * rows, :] = (base + local[chunk, j]).astype(jnp.bfloat16)
        for tile in range(hidden // HID_TILE):
            cols = slice(tile * HID_TILE, (tile + 1) * HID_TILE)
            pre = jnp.dot(state[...], w_in[:, cols], preferred_element_type=jnp.float32)
            for j in range(both):
                activate(pre[j * rows:(j + 1) * rows], j, cols)
        tx[0, turn] = drifts(chunk)
        send(0, chunk, turn)
        exchange(turn, True, step_index)
        return carry

    lax.fori_loop(0, CHUNKS, first_chunk, 0)
    lax.fori_loop(CHUNKS, NUM_SWEEPS * CHUNKS, later_chunk, 0)

    def local_copy(chunk):
        return pltpu.make_async_remote_copy(
            src_ref=local.at[chunk, pl.ds((1 - core) * steps, steps)], dst_ref=sib_local.at[chunk], send_sem=loc_send.at[chunk],
            recv_sem=loc_recv.at[chunk], device_id=at(sibling), device_id_type=MESH)

    def before_copy(chunk):
        return pltpu.make_async_remote_copy(
            src_ref=before.at[chunk], dst_ref=sib_before.at[chunk], send_sem=bef_send.at[chunk],
            recv_sem=bef_recv.at[chunk], device_id=at(sibling), device_id_type=MESH)

    def give(chunk):
        span = slice(chunk * rows, (chunk + 1) * rows)
        local_copy(chunk).wait()
        before_copy(chunk).wait()
        mine = x_ref[core, span, :] + before[chunk]
        theirs = x_ref[1 - core, span, :] + sib_before[chunk]
        for j in range(steps):
            out_ref[j, core, span, :] = mine + local[chunk, core * steps + j]
            out_ref[j, 1 - core, span, :] = theirs + sib_local[chunk, j]

    for chunk in range(CHUNKS):
        local_copy(chunk).start()
    before_copy(0).start()
    finish(0, 3, 1)
    finish(1, 2, 0)
    finish(2, 1, 1)
    before_copy(1).start()
    give(0)
    finish(1, 3, 1)
    finish(2, 2, 0)
    before_copy(2).start()
    give(1)
    give(2)
    finish(2, 3, 1)
    before_copy(3).start()
    give(3)


def solution(mesh):
    num_time = mesh.shape["time"]
    side = round((num_time // 2) ** (1 / 3))

    def body(x_init, w_in, w_out, gamma_c, beta_c, gamma_u, beta_u, step_h, guide_w):
        samples, tokens, channels = x_init.shape
        hidden = w_in.shape[1]
        steps = step_h.shape[0]
        rows = tokens // CHUNKS
        both = 2 * steps
        f32, bf16 = jnp.float32, jnp.bfloat16
        vmem = pl.BlockSpec(memory_space=pltpu.VMEM)
        smem = pl.BlockSpec(memory_space=pltpu.SMEM)
        dma = pltpu.SemaphoreType.DMA
        hops = side - 1
        return pl.pallas_call(
            functools.partial(sampler, (steps, rows, channels, hidden, side)),
            out_shape=jax.ShapeDtypeStruct((steps, samples, tokens, channels), f32),
            in_specs=[vmem] * 7 + [smem] * 2,
            out_specs=vmem,
            scratch_shapes=[
                pltpu.VMEM((CHUNKS, both, rows, channels), f32),
                pltpu.VMEM((CHUNKS, steps, rows, channels), f32),
                pltpu.VMEM((CHUNKS, rows, channels), f32),
                pltpu.VMEM((CHUNKS, rows, channels), f32),
                pltpu.VMEM((both * rows, channels), bf16),
                pltpu.VMEM((2 * both * rows, hidden), bf16),
                pltpu.VMEM((tokens, hidden), f32),
                pltpu.VMEM((4, both, hidden), f32),
                pltpu.VMEM((4, steps, hidden), bf16),
                pltpu.VMEM((2, both, channels), f32),
                pltpu.VMEM((2, steps, channels), f32),
                pltpu.VMEM((2, steps, channels), f32),
                pltpu.VMEM((3, 2, rows, channels), f32),
                pltpu.VMEM((3, CHUNKS, hops, rows, channels), f32),
                dma((3, 2, hops)), dma((3, CHUNKS, hops)),
                dma((4,)), dma((4,)), dma, dma,
                dma((CHUNKS,)), dma((CHUNKS,)), dma((CHUNKS,)), dma((CHUNKS,)),
            ],
            compiler_params=pltpu.CompilerParams(collective_id=0, has_side_effects=True, vmem_limit_bytes=62 * 2 ** 20),
            name="picard_sampler",
        )(x_init, w_in, w_out, gamma_c, beta_c, gamma_u, beta_u, step_h, guide_w)

    return jax.shard_map(body, mesh=mesh, in_specs=(P("data", None, None), P(None, None), P(None, None), P("time", None), P("time", None), P("time", None), P("time", None), P("time"), P(None)), out_specs=P("time", "data", None, None), check_vma=False)
```

time: 589 us -> 153 us (0.26)
  starting transfers between devices: 214 us -> 0 us
  matrix products: 171 us -> 0 us
  Pallas kernels: 0 us -> 146 us
  waiting for transfers between devices: 141 us -> 0 us
  other arithmetic: 47.3 us -> 0 us
  local copies, waits for them, and re-layouts: 13.6 us -> 4.98 us
    ppermute x28 -> x0, starting transfers between devices: 214 us -> none  [sweep(): prefix = prefix + lax.ppermute(prefix, 'time', perm)]
    dot_general x8 -> x0, matrix products: 171 us -> none  [the longest x4 113 us: sweep(): jnp.einsum('ekbnd,dc->ekbnc', act, w_out, preferred_element_type=jnp.floa...]
    pallas_call x0 -> x1, Pallas kernels: none -> 146 us  [body(): pl.pallas_call(functools.partial(sampler, (steps, rows, channels, hidden,...]
    ppermute x28 -> x0, waiting for transfers between devices: 141 us -> none  [sweep(): prefix = prefix + lax.ppermute(prefix, 'time', perm)]
    add x29 -> x0, other arithmetic: 22.2 us -> none  [the longest x4 20 us: sweep(): return x_init[None] + (before[None] + local_before)]
    another operation x4 -> x0, other arithmetic: 19.8 us -> none  [sweep(): running = jnp.cumsum(drift, axis=0)]
    slice x4 -> x0, local copies, waits for them, and re-layouts: 9.71 us -> none  [sweep(): running[:-1]]
  transfers between devices with their start and end apart: 28 -> 0, of which waited for: 28 -> 0; matrix products, arithmetic and copies ran while one was open for 2% -> 0% of each run, Pallas kernels for 0% -> 0%
where the time goes in v1:
time: 153 us; the launch traced here: 152 us
  Pallas kernels  146 us (95%)
  local copies, waits for them, and re-layouts  4.98 us (3%)
    pallas_call x1, Pallas kernels, body(): pl.pallas_call(functools.partial(sampler, (steps, rows, channels, hidden,...  146 us
    unnamed x1, local copies, waits for them, and re-layouts  4.98 us

profile of v1, /device:TPU:0, one launch (start us, length us, event | category | flops | bytes accessed | tf_op | source)
XLA Modules:
  0.0 151.6 jit_solution(15654259757061316702)
XLA Ops:
  0.7 146.0 %picard_sampler.1 = f32[12,2,64,768]{3,2,1,0:T(8,128)} custom-call(f32[2,64,768]{2,1,0:T(8,128)} %x_ref.1, bf16[768,3072]{1,0:T(8,128)(2,1)} %w_in.1, bf16[3072,768]{1,0:T(8,128)(2,1)} %w_out.1, bf16[12,3072]{1,0:T(8,128)(2,1)} %gamma_c.1, bf16[12,3072]{1,0:T(8,128)(2,1)} %beta_c.1, bf16[12,3072]{1,0:T(8,128)(2,1)} %gamma_u.1, bf16[12,3072]{1,0:T(8,128)(2,1)} %beta_u.1, ...), custom_call_target="tpu_custom_call" | custom-call | tf_op jit(solution)/shard_map/picard_sampler/pallas_call | solution.py:219
  146.6 5.0 %copy.12 = f32[12,2,64,768]{3,2,1,0:T(8,128)} copy(f32[12,2,64,768]{3,2,1,0:T(8,128)} %picard_sampler.1) | data formatting | bytes 9437184
